TPU v7x, 32 devices: a whole 2x2x4 slice. The times are simulated.
32 devices in a mesh: groups: 2 (over y), ep: 4 (over z), dp: 4 (over x, core), tp: 1.
Axes of the slice: x: 2, y: 2, z: 4, core: 2. Of those that a mesh axis runs over, the one named last changes fastest.
Arguments:
- tokens: bfloat16 [2048, 2048], P(('groups', 'ep', 'dp', 'tp')), parts along dimension 0, may hold values from -6 to 6
- experts_one: int32 [2048, 8], P(('groups', 'ep', 'dp', 'tp')), parts along dimension 0, may hold values from 0 to 15, all different within a row; in each aligned block of 64 rows (0 to 63, 64 to 127, ...) at most 40 rows name the same one
- gates_one: float32 [2048, 8], P(('groups', 'ep', 'dp', 'tp')), parts along dimension 0, may hold values from 0.05 to 0.5
- w_in_one: bfloat16 [16, 2048, 2, 768], P(('ep', 'dp'), None, None, 'tp'), may hold values from -0.125 to 0.125
- w_down_one: bfloat16 [16, 768, 2048], P(('ep', 'dp'), 'tp'), may hold values from -0.21875 to 0.21875
- norm_gain: float32 [2048], replicated, may hold values from 0.5 to 1.5
- experts_two: int32 [2048, 8], P(('groups', 'ep', 'dp', 'tp')), parts along dimension 0, may hold values from 0 to 15, all different within a row; in each aligned block of 64 rows (0 to 63, 64 to 127, ...) at most 40 rows name the same one
- gates_two: float32 [2048, 8], P(('groups', 'ep', 'dp', 'tp')), parts along dimension 0, may hold values from 0.05 to 0.5
- placement_two: int32 [16], replicated, may hold values from 0 to 15, each once
- w_in_two: bfloat16 [16, 2048, 2, 768], P(('ep', 'dp'), None, None, 'tp'), may hold values from -0.125 to 0.125
- w_down_two: bfloat16 [16, 768, 2048], P(('ep', 'dp'), 'tp'), may hold values from -0.21875 to 0.21875
Outputs:
- layer_out: bfloat16 [2048, 2048], P(('groups', 'ep', 'dp', 'tp')), parts along dimension 0
There are 2 independent parts, one for each index of `groups`. A program takes and returns all parts, laid end to end along the dimension named above; an argument that names none is the same for every part. Nothing has to cross between parts.
Inputs may be any that keep to these rules, and one draw needn't show every extreme that they name: `experts_one`: each token names 8 different experts; among the 64 tokens of one device no expert is named more than 40 times, and on some device some expert is named exactly 40 times. `experts_two`: each token names 8 different experts; among the 64 tokens of one device no expert is named more than 40 times, and on some device some expert is named exactly 40 times. `placement_two`: each slot is named by exactly one expert.
All inputs are finite; a program needn't handle non-finite values.
Results may differ from a plain program's by a relative error of at most 0.011.
Values may be sent and summed in bfloat16 or wider, within the bound.
A program may use at most 128 MiB of HBM per device.

v0:
```python
import functools

import jax
import jax.numpy as jnp
from jax import lax
from jax.experimental import pallas as pl
from jax.experimental.pallas import tpu as pltpu
from jax.sharding import PartitionSpec as P

MESH = pl.DeviceIdType.MESH
LANES = 128


def layer_kernel(
    n, experts, width, blk, w_in_hbm, w_down_hbm, out,
    rows, part, core_in, cross, x_in, line, z_in, raw, w_in, w_down, hidden,
    w_sem, z_send, z_recv, x_send, x_recv, c_send, c_recv, d_send, d_recv,
    rc_send, rc_recv, rx_send, rx_recv, rz_send, rz_recv,
):
    z = lax.axis_index("ep")
    d = lax.axis_index("dp")
    mine = z * lax.axis_size("dp") + d
    x_peer = {"dp": (d + 2) % 4}
    c_peer = {"dp": d + 1 - 2 * (d % 2)}
    half = w_down.shape[0]
    tok = blk.shape[0]
    pair = z + 1 - 2 * (z % 2)
    order = [z, pair, 2 - z // 2, 3 - 3 * (z // 2)]
    inner = z % 3 != 0

    def remote(src, dst, send, recv, to):
        return pltpu.make_async_remote_copy(
            src_ref=src, dst_ref=dst, send_sem=send, recv_sem=recv, device_id=to, device_id_type=MESH
        )

    load_in = pltpu.make_async_copy(w_in_hbm, raw, w_sem.at[0])
    load_down = pltpu.make_async_copy(w_down_hbm, w_down, w_sem.at[1])
    load_in.start()
    load_down.start()

    barrier = pltpu.get_barrier_semaphore()
    for k in range(1, n):
        pl.semaphore_signal(barrier, inc=1, device_id={"ep": (z + k) % n}, device_id_type=MESH)
    pl.semaphore_signal(barrier, inc=1, device_id=x_peer, device_id_type=MESH)
    pl.semaphore_signal(barrier, inc=1, device_id=c_peer, device_id_type=MESH)
    pl.semaphore_wait(barrier, n + 1)

    sends = []

    def go(copy):
        copy.start()
        sends.append(copy)
        return copy

    size = tok // 2
    halves = [pl.ds(h * size, size) for h in range(2)]
    has_up, has_down = z < n - 1, z > 0
    outer = jnp.logical_not(inner)
    ups, downs = [], []
    for h, at in enumerate(halves):
        own = blk.at[at]
        ups.append(remote(own, rows.at[z, 0, at], z_send.at[0, h], z_recv.at[z, h], {"ep": (z + 1) % n}))
        downs.append(remote(own, rows.at[z, 0, at], z_send.at[n, h], z_recv.at[z, h], {"ep": (z + n - 1) % n}))
    x_copy, c_copy, d_copy = {}, {}, {}
    for i, b in enumerate(order):
        src = blk if i == 0 else rows.at[b, 0]
        for h, at in enumerate(halves):
            x_copy[i, h] = remote(src.at[at], rows.at[b, 1, at], x_send.at[i, h], x_recv.at[i, h], x_peer)
        c_copy[i] = remote(src, rows.at[b, 2], c_send.at[i], c_recv.at[i], c_peer)
        d_copy[i] = remote(rows.at[b, 1], rows.at[b, 3], d_send.at[i], d_recv.at[i], c_peer)
        sends += [x_copy[i, 0], x_copy[i, 1], c_copy[i], d_copy[i]]

    def arrive(i, relay):
        b = order[i]
        to = {"ep": 3 - z if i == 1 else pair}
        for h, at in enumerate(halves):
            move = remote(rows.at[b, 0, at], rows.at[b, 0, at], z_send.at[i, h], z_recv.at[b, h], to)
            move.wait_recv()
            if relay:
                pl.when(inner)(move.start)
            x_copy[i, h].start()
        c_copy[i].start()

    for h in range(2):
        pl.when(has_up)(ups[h].start)
        pl.when(has_down)(downs[h].start)
        x_copy[0, h].start()
    c_copy[0].start()
    rows[z, 0] = blk[...]
    rc_copy, rx_copy = {}, {}

    def to_cross(i):
        rc_copy[i].wait_recv()
        for h, at in enumerate(halves):
            value = part[i, 1, at].astype(jnp.float32) + core_in[i, 1, at].astype(jnp.float32)
            cross[i, at] = value.astype(cross.dtype)
            rx_copy[i, h] = go(
                remote(cross.at[i, at], x_in.at[i, at], rx_send.at[i, h], rx_recv.at[i, h], x_peer)
            )

    def finish(i):
        for h, at in enumerate(halves):
            rx_copy[i, h].wait_recv()
            total = (
                part[i, 0, at].astype(jnp.float32)
                + core_in[i, 0, at].astype(jnp.float32)
                + x_in[i, at].astype(jnp.float32)
            )
            if i == 0:
                out[at] = total
            else:
                line[i, at] = total.astype(line.dtype)
                go(remote(line.at[i, at], z_in.at[z, at], rz_send.at[i, h], rz_recv.at[z, h], {"ep": order[i]}))

    for i, b in enumerate(order):
        if i == 0:
            arrive(1, True)
            pl.when(inner)(functools.partial(arrive, 2, True))
        elif i == 1:
            pl.when(outer)(functools.partial(arrive, 2, False))
            pl.when(inner)(functools.partial(arrive, 3, True))
        elif i == 2:
            pl.when(outer)(functools.partial(arrive, 3, False))
        for h in range(2):
            x_copy[i, h].wait_recv()
        d_copy[i].start()
        if i == 0:
            load_in.wait()
            group = 128

            @pl.loop(0, w_in.shape[0] // group)
            def _(j):
                at = pl.ds(pl.multiple_of(j * group, group), group)
                w_in[at] = raw[at].reshape(group, 2 * half)

            load_down.wait()
        c_copy[i].wait_recv()
        d_copy[i].wait_recv()
        gates = rows[b, :, :, width:].reshape(4 * tok, LANES).astype(jnp.float32)
        lane = lax.broadcasted_iota(jnp.int32, (4 * tok, LANES), 1)
        weight = jnp.sum(jnp.where((lane == mine) | (lane == mine + experts), gates, 0.0), axis=1, keepdims=True)
        step = 256 if half % 256 == 0 else LANES

        @pl.loop(0, half // step)
        def _(j):
            x = rows[b, :, :, :width].reshape(4 * tok, width)
            at = pl.multiple_of(j * step, step)
            gate = jnp.dot(x, w_in[:, pl.ds(at, step)], preferred_element_type=jnp.float32)
            up_part = jnp.dot(x, w_in[:, pl.ds(half + at, step)], preferred_element_type=jnp.float32)
            hidden[:, pl.ds(at, step)] = (gate / (1.0 + jnp.exp(-gate)) * up_part).astype(hidden.dtype)

        y = jnp.dot(hidden[...], w_down[...], preferred_element_type=jnp.float32)
        y = jnp.where(weight == 0.0, 0.0, y * weight)
        part[i] = y.astype(part.dtype).reshape(4, tok, width)

        rc_copy[i] = go(remote(part.at[i, pl.ds(2, 2)], core_in.at[i], rc_send.at[i], rc_recv.at[i], c_peer))
        if i > 0:
            to_cross(i)
        if i == n - 1:
            to_cross(0)
        if i > 1:
            finish(i - 1)
    finish(n - 1)
    finish(0)
    for i in range(1, n):
        b = order[i]
        for h, at in enumerate(halves):
            remote(line.at[i, at], z_in.at[b, at], rz_send.at[0, h], rz_recv.at[b, h], {"ep": b}).wait_recv()
            out[at] += z_in[b, at].astype(jnp.float32)
    for h in range(2):
        pl.when(has_up)(ups[h].wait_send)
        pl.when(has_down)(downs[h].wait_send)
    for i in range(1, n):
        for h, at in enumerate(halves):
            spot = rows.at[order[i], 0, at]
            pl.when(inner)(remote(spot, spot, z_send.at[i, h], z_recv.at[0, h], {"ep": pair}).wait_send)
    for copy in sends:
        copy.wait_send()


def expert_layer(block, w_in, w_down, experts, number):
    tok, wide = block.shape
    half, width = w_down.shape[1:]
    n = lax.axis_size("ep")
    bf16 = jnp.bfloat16
    dma = pltpu.SemaphoreType.DMA
    return pl.pallas_call(
        functools.partial(layer_kernel, n, experts, width),
        out_shape=jax.ShapeDtypeStruct((tok, width), jnp.float32),
        in_specs=[
            pl.BlockSpec(memory_space=pltpu.VMEM),
            pl.BlockSpec(memory_space=pl.ANY),
            pl.BlockSpec(memory_space=pl.ANY),
        ],
        out_specs=pl.BlockSpec(memory_space=pltpu.VMEM),
        scratch_shapes=[
            pltpu.VMEM((n, 4, tok, wide), bf16),
            pltpu.VMEM((n, 4, tok, width), bf16),
            pltpu.VMEM((n, 2, tok, width), bf16),
            pltpu.VMEM((n, tok, width), bf16),
            pltpu.VMEM((n, tok, width), bf16),
            pltpu.VMEM((n, tok, width), bf16),
            pltpu.VMEM((n, tok, width), bf16),
            pltpu.VMEM((width, 2, half), bf16),
            pltpu.VMEM((width, 2 * half), bf16),
            pltpu.VMEM((half, width), bf16),
            pltpu.VMEM((4 * tok, half), bf16),
            dma((2,)),
            dma((n + 1, 2)),
            dma((n, 2)),
            dma((n, 2)),
            dma((n, 2)),
        ]
        + [dma((n,))] * 6
        + [dma((n, 2))] * 4,
        compiler_params=pltpu.CompilerParams(
            collective_id=number, has_side_effects=True, vmem_limit_bytes=56 * 1024 * 1024
        ),
        name=f"layer_{number}",
    )(block, w_in.reshape(width, 2, half), w_down.reshape(half, width))


def with_gates(rows_in, targets, gate_values, experts):
    matches = targets[:, :, None] == jnp.arange(experts, dtype=jnp.int32)[None, None, :]
    table = jnp.sum(jnp.where(matches, gate_values[:, :, None], 0.0), axis=1)
    high = table.astype(jnp.bfloat16)
    low = (table - high.astype(jnp.float32)).astype(jnp.bfloat16)
    rest = jnp.zeros((rows_in.shape[0], LANES - 2 * experts), jnp.bfloat16)
    return jnp.concatenate([rows_in, high, low, rest], axis=1)


def fused_shards(
    tokens, experts_one, gates_one, w_in_one, w_down_one, norm_gain,
    experts_two, gates_two, placement_two, w_in_two, w_down_two,
):
    experts = placement_two.shape[0]
    expert_range = jnp.arange(experts, dtype=jnp.int32)
    matches = experts_two[:, :, None] == expert_range[None, None, :]
    layer_slots = jnp.sum(jnp.where(matches, placement_two[None, None, :], 0), axis=2)
    moe_one = expert_layer(with_gates(tokens, experts_one, gates_one, experts), w_in_one, w_down_one, experts, 0)
    mixed = (tokens.astype(jnp.float32) + moe_one).astype(jnp.bfloat16)
    mixed_wide = mixed.astype(jnp.float32)
    inv_rms = lax.rsqrt(jnp.mean(mixed_wide * mixed_wide, axis=1, keepdims=True) + 1e-06)
    normed = (mixed_wide * inv_rms * norm_gain[None, :]).astype(jnp.bfloat16)
    moe_two = expert_layer(with_gates(normed, layer_slots, gates_two, experts), w_in_two, w_down_two, experts, 1)
    return (mixed_wide + moe_two).astype(jnp.bfloat16)


def capacity(tok_rows, top_count, expert_count):
    return max(2, min(tok_rows, 5 * tok_rows * top_count // (4 * expert_count)))


def pack_rows(rows_in, targets, expert_count, per_slot):
    tok_rows, top_count = targets.shape
    flat_ids = targets.reshape(-1)
    hit_table = (flat_ids[:, None] == jnp.arange(expert_count, dtype=jnp.int32)[None, :]).astype(
        jnp.int32
    )
    before = jnp.cumsum(hit_table, axis=0) - hit_table
    slot_rank = jnp.sum(before * hit_table, axis=1)
    slot_index = flat_ids * per_slot + slot_rank
    source = jnp.arange(tok_rows * top_count, dtype=jnp.int32) // top_count
    owner_row = jnp.zeros((expert_count * per_slot,), jnp.int32).at[slot_index].set(source)
    filled = jnp.zeros((expert_count * per_slot,), jnp.int32).at[slot_index].set(1)
    buffer = jnp.where(filled[:, None] > 0, rows_in[owner_row], jnp.zeros((), rows_in.dtype))
    return (buffer, slot_index)


def to_experts(buffer, expert_count, per_slot):
    row_width = buffer.shape[1]
    arrived = lax.all_to_all(
        buffer.reshape(expert_count, per_slot, row_width),
        ("ep", "dp"),
        split_axis=0,
        concat_axis=0,
        tiled=True,
    )
    return arrived.reshape(expert_count * per_slot, row_width)


def to_owners(produced, expert_count, per_slot):
    row_width = produced.shape[1]
    returned = lax.all_to_all(
        produced.reshape(expert_count, per_slot, row_width),
        ("ep", "dp"),
        split_axis=0,
        concat_axis=0,
        tiled=True,
    )
    return returned.reshape(expert_count * per_slot, row_width)


def run_expert(received, w_in, w_down):
    row_width = received.shape[1]
    down_local = w_down[0]
    half_width = down_local.shape[0]
    w_local = w_in.reshape(row_width, 2 * half_width)
    gate_up = jnp.dot(
        lax.all_gather(received, "tp", axis=0, tiled=True),
        w_local,
        preferred_element_type=jnp.float32,
    )
    hidden = (jax.nn.silu(gate_up[:, :half_width]) * gate_up[:, half_width:]).astype(jnp.bfloat16)
    return lax.psum_scatter(
        jnp.dot(hidden, down_local, preferred_element_type=jnp.float32).astype(jnp.bfloat16),
        "tp",
        scatter_dimension=0,
        tiled=True,
    )


def moe_block(rows_in, targets, gate_values, w_in, w_down, expert_count, per_slot):
    tok_rows, top_count = targets.shape
    row_width = rows_in.shape[1]
    buffer, slot_index = pack_rows(rows_in, targets, expert_count, per_slot)
    arrived = to_experts(buffer, expert_count, per_slot)
    produced = run_expert(arrived, w_in, w_down)
    returned = to_owners(produced, expert_count, per_slot)
    picked = returned[slot_index].reshape(tok_rows, top_count, row_width)
    return jnp.sum(gate_values[:, :, None] * picked.astype(jnp.float32), axis=1)


def shards(
    tokens,
    experts_one,
    gates_one,
    w_in_one,
    w_down_one,
    norm_gain,
    experts_two,
    gates_two,
    placement_two,
    w_in_two,
    w_down_two,
):
    tok_rows, top_count = experts_one.shape
    expert_count = placement_two.shape[0]
    per_slot = capacity(tok_rows, top_count, expert_count)
    moe_one = moe_block(
        tokens, experts_one, gates_one, w_in_one, w_down_one, expert_count, per_slot
    )
    mixed = (tokens.astype(jnp.float32) + moe_one).astype(jnp.bfloat16)
    mixed = lax.optimization_barrier(mixed)
    mixed_wide = mixed.astype(jnp.float32)
    inv_rms = lax.rsqrt(jnp.mean(mixed_wide * mixed_wide, axis=1, keepdims=True) + 1e-06)
    normed = (mixed_wide * inv_rms * norm_gain[None, :]).astype(jnp.bfloat16)
    expert_range = jnp.arange(expert_count, dtype=jnp.int32)
    matches = experts_two[:, :, None] == expert_range[None, None, :]
    layer_slots = jnp.sum(jnp.where(matches, placement_two[None, None, :], 0), axis=2)
    moe_two = moe_block(
        normed, layer_slots, gates_two, w_in_two, w_down_two, expert_count, per_slot
    )
    return (mixed_wide + moe_two).astype(jnp.bfloat16)


def solution(mesh):
    in_specs = (
        P(("groups", "ep", "dp", "tp"), None),
        P(("groups", "ep", "dp", "tp"), None),
        P(("groups", "ep", "dp", "tp"), None),
        P(("ep", "dp"), None, None, "tp"),
        P(("ep", "dp"), "tp", None),
        P(),
        P(("groups", "ep", "dp", "tp"), None),
        P(("groups", "ep", "dp", "tp"), None),
        P(),
        P(("ep", "dp"), None, None, "tp"),
        P(("ep", "dp"), "tp", None),
    )
    out_specs = P(("groups", "ep", "dp", "tp"), None)
    ready = mesh.shape["tp"] == 1 and mesh.shape["dp"] == 4 and mesh.shape["ep"] == 4

    def body(*arrays):
        return (fused_shards if ready and arrays[0].shape[0] % 32 == 0 else shards)(*arrays)

    return jax.shard_map(body, mesh=mesh, in_specs=in_specs, out_specs=out_specs, check_vma=False)
```

profile of v0, /device:TPU:0, one launch (start us, length us, event | category | flops | bytes accessed | tf_op | source)
XLA Modules:
  0.0 142.0 jit_solution(4362707304191840145)
XLA Ops:
  0.0 0.0 copy-start
  0.0 0.0 copy-start.1
  0.0 0.8 select_reduce_fusion.1
  0.8 0.7 select_reduce_fusion
  1.6 0.7 select_reduce_fusion.2
  2.3 0.1 copy.22
  2.4 0.1 copy.25
  2.5 0.1 copy.21
  2.6 0.1 copy.24
  2.7 1.7 %concatenate.6.blk = bf16[64,2176]{1,0:T(8,128)(2,1)} concatenate(bf16[64,2048]{1,0:T(8,128)(2,1)} %param.11, bf16[64,16]{1,0:T(8,128)(2,1)S(1)} %copy.22, bf16[64,16]{1,0:T(8,128)(2,1)S(1)} %subtract_convert_fusion.1, bf16[64,96]{1,0:T(8,128)(2,1)S(1)} %broadcast.21), dimensions={1} | concatenate | bytes 557056 | tf_op jit(solution)/shard_map/concatenate | solution.py:229
  4.4 69.5 %layer_0.1 = f32[64,2048]{1,0:T(8,128)} custom-call(bf16[64,2176]{1,0:T(8,128)(2,1)} %concatenate.6.blk, bf16[2048,2,768]{2,1,0:T(2,128)(2,1)} %bitcast.4, bf16[768,2048]{1,0:T(8,128)(2,1)} %bitcast.6), custom_call_target="tpu_custom_call" | custom-call | tf_op jit(solution)/shard_map/layer_0/pallas_call | solution.py:187
  74.0 0.0 copy-done
  74.0 1.2 fusion
  75.2 0.0 copy-done.1
  75.2 0.1 fusion.2
  75.4 0.8 concatenate.7.blk
  76.2 64.1 %layer_1.1 = f32[64,2048]{1,0:T(8,128)} custom-call(bf16[64,2176]{1,0:T(8,128)(2,1)} %concatenate.7.blk, bf16[2048,2,768]{2,1,0:T(2,128)(2,1)} %bitcast.5, bf16[768,2048]{1,0:T(8,128)(2,1)} %bitcast.7), custom_call_target="tpu_custom_call" | custom-call | tf_op jit(solution)/shard_map/layer_1/pallas_call | solution.py:187
  140.2 1.8 %fusion.3 = bf16[64,2048]{1,0:T(8,128)(2,1)} fusion(f32[64,2048]{1,0:T(8,128)} %layer_1.1, bf16[64,2048]{1,0:T(8,128)(2,1)S(1)} %get-tuple-element.6), kind=kLoop, calls=%fused_computation.6 | loop fusion | flops 393216 | bytes 1048576 | tf_op jit(solution)/shard_map/convert_element_type | solution.py:246
  (6 shorter events, 0.0 us)
Async XLA Ops:
  0.0 74.0 %copy-start = (bf16[64,2048]{1,0:T(8,128)(2,1)S(1)}, bf16[64,2048]{1,0:T(8,128)(2,1)}, u32[]{:S(2)}) copy-start(bf16[64,2048]{1,0:T(8,128)(2,1)} %param.11) | copy-start | bytes 786436
  0.0 75.2 %copy-start.1 = (f32[2048]{0:T(1024)S(1)}, f32[2048]{0:T(1024)}, u32[]{:S(2)}) copy-start(f32[2048]{0:T(1024)} %param.16) | copy-start | bytes 24580
where the time goes:
time: 142 us
  Pallas kernels  134 us (94%)
  other arithmetic  5.44 us (4%)
  local copies, waits for them, and re-layouts  2.92 us (2%)
    pallas_call x2, Pallas kernels, expert_layer(): pl.pallas_call(functools.partial(layer_kernel, n, experts, width), out_sh...  134 us

commit v1 on v0

v1 whole, which is shorter than its diff:
```python
import functools

import jax
import jax.numpy as jnp
from jax import lax
from jax.experimental import pallas as pl
from jax.experimental.pallas import tpu as pltpu
from jax.sharding import PartitionSpec as P

MESH = pl.DeviceIdType.MESH
LANES = 128


STREAMS = 2
PIECES = 2
GATHER = ('zx', 'zx')
REDUCE = ('zz', 'zz')
PROGRAM = (
    "S00 W0 S01 W1",
    "x000 a002 a001 x010",
    "a011 C000 a003 x002",
    "C010 k000 C002 x001",
    "b012 k010 b011 x003",
    "k002 a012 C001 C003",
    "a013 C012 k003 b013",
    "t002 k012 k001 C013",
    "t003 C011 t012 t000",
    "k013 t001 k011 t013",
    "F00 t011 t010 a101",
    "x100 a102 F01 x101",
    "C101 x102 a103 C100",
    "x110 C102 x103 k101",
    "a111 a112 k100 C103",
    "b112 k103 a113 b111",
    "C112 k102 b113 t103",
    "k112 C113 t102 t101",
    "k113 C111 C110 k111",
    "t100 t113 k110 t112",
    "t111 F10 t110 F11",
)


def fused_kernel(
    n, experts, width, tokens_hbm, experts_hbm, gates_hbm, experts2_hbm, gates2_hbm, gain_ref, place, w_in1, w_down1,
    w_in2, w_down2, out, tokens, ids, gates, mixed, rows1, rows2, part, core_in, cross, x_in, z_in, raw, w_in, w_down,
    hidden, w_sem, z_send, z_recv, x_send, x_recv, c_send, c_recv, rc_send, rc_recv, rx_send, rx_recv, rz_send, rz_recv,
):
    z = lax.axis_index("ep")
    d = lax.axis_index("dp")
    mine = z * lax.axis_size("dp") + d
    x_peer = {"dp": (d + 2) % 4}
    c_peer = {"dp": d + 1 - 2 * (d % 2)}
    half = w_down.shape[1]
    tok = tokens.shape[0]
    size = tok // STREAMS
    pair = z + 1 - 2 * (z % 2)
    other = 3 - z
    order = [z, pair, 2 - z // 2, 3 - 3 * (z // 2)]
    inner = z % 3 != 0
    outer = jnp.logical_not(inner)
    rows = [rows1, rows2]
    f32, bf16 = jnp.float32, jnp.bfloat16
    cut = size // PIECES
    at = [pl.ds(p * cut, cut) for p in range(PIECES)]

    def remote(src, dst, send, recv, to):
        return pltpu.make_async_remote_copy(
            src_ref=src, dst_ref=dst, send_sem=send, recv_sem=recv, device_id=to, device_id_type=MESH
        )

    small = [
        pltpu.make_async_copy(src, dst, w_sem.at[k])
        for k, (src, dst) in enumerate(
            [
                (tokens_hbm, tokens), (experts_hbm, ids.at[0]), (gates_hbm, gates.at[0]),
                (experts2_hbm, ids.at[1]), (gates2_hbm, gates.at[1]),
            ]
        )
    ]
    load_in = [pltpu.make_async_copy(w, raw, w_sem.at[5 + k]) for k, w in enumerate((w_in1, w_in2))]
    load_down = [pltpu.make_async_copy(w, w_down.at[k], w_sem.at[7 + k]) for k, w in enumerate((w_down1, w_down2))]
    for copy in small + [load_in[0], load_down[0], load_down[1]]:
        copy.start()

    barrier = pltpu.get_barrier_semaphore()
    pl.semaphore_signal(barrier, inc=1, device_id={"ep": pair}, device_id_type=MESH)
    pl.semaphore_signal(barrier, inc=1, device_id=x_peer, device_id_type=MESH)
    pl.semaphore_signal(barrier, inc=1, device_id=c_peer, device_id_type=MESH)

    @pl.when(inner)
    def _():
        pl.semaphore_signal(barrier, inc=1, device_id={"ep": other}, device_id_type=MESH)

    sends = []

    def go(copy, when=None):
        if when is None:
            copy.start()
        else:
            pl.when(when)(copy.start)
        sends.append((copy, when))

    for copy in small:
        copy.wait()
    lane = lax.broadcasted_iota(jnp.int32, (LANES, tok), 0)
    table = jnp.zeros((LANES, tok), f32)
    for l in range(2):
        here = jnp.where(lane // (2 * experts) == l, lane % experts, -1)
        for k in range(ids.shape[1]):
            table += jnp.where(ids[l, k : k + 1] == here, gates[l, k : k + 1], 0.0)
    high = table.astype(bf16).astype(f32)
    table = jnp.where((lane // experts) % 2 == 0, high, table - high).T.astype(bf16)
    for s in range(STREAMS):
        own = pl.ds(s * size, size)
        rows1[s, z, 0, :, :width] = tokens[own]
        rows1[s, z, 0, :, width:] = table[s * size : (s + 1) * size]
    e_mine = 0
    for e in range(experts):
        e_mine = e_mine + jnp.where(place[e] == mine, e, 0)
    lanes = [mine, 2 * experts + e_mine]

    @pl.when(inner)
    def _():
        pl.semaphore_wait(barrier, 4)

    @pl.when(outer)
    def _():
        pl.semaphore_wait(barrier, 3)

    def block(l, s, b, j):
        return rows[l].at[s, b, j]

    def z_own(l, s, j):
        q = 2 * l + s
        for p in range(PIECES):
            spot = block(l, s, z, j).at[at[p]]
            up = remote(spot, spot, z_send.at[q, 0, j, p], z_recv.at[q, z, j, p], {"ep": pair})
            go(up)
            down = remote(spot, spot, z_send.at[q, 1, j, p], z_recv.at[q, z, j, p], {"ep": other})
            go(down, inner)

    def x_move(l, s, i):
        q, b = 2 * l + s, order[i]
        for p in range(PIECES):
            go(
                remote(
                    block(l, s, b, 0).at[at[p]], block(l, s, b, 1).at[at[p]], x_send.at[q, i, p], x_recv.at[q, i, p], x_peer
                )
            )

    def c_move(l, s, i, j):
        q, b = 2 * l + s, order[i]
        go(remote(block(l, s, b, j), block(l, s, b, 2 + j), c_send.at[q, i, j], c_recv.at[q, i, j], c_peer))

    def start(l, s):
        z_own(l, s, 0)
        x_move(l, s, 0)
        c_move(l, s, 0, 0)

    def arrive(j, l, s, i):
        q, b = 2 * l + s, order[i]
        to = {"ep": other if i == 1 else pair}
        first = GATHER[l][s] == "z"
        if first and j == 1:
            return
        for p in range(PIECES):
            spot = block(l, s, b, j).at[at[p]]
            move = remote(spot, spot, z_send.at[q, 1 + i, j, p], z_recv.at[q, b, j, p], to)
            move.wait_recv()
            go(move, inner)
            if first:
                go(
                    remote(spot, block(l, s, b, 1).at[at[p]], x_send.at[q, i, p], x_recv.at[q, i, p], x_peer)
                )
        c_move(l, s, i, j)

    def x_arrive(l, s, i):
        if GATHER[l][s] == "x" and i > 0:
            return
        q, b = 2 * l + s, order[i]
        for p in range(PIECES):
            spot = block(l, s, b, 1).at[at[p]]
            remote(spot, spot, x_send.at[q, i, p], x_recv.at[q, i, p], x_peer).wait_recv()
        if GATHER[l][s] == "x":
            z_own(l, s, 1)
        c_move(l, s, i, 1)

    def weights(l):
        load_in[l].wait()
        group = 128

        @pl.loop(0, width // group)
        def _(j):
            here = pl.ds(pl.multiple_of(j * group, group), group)
            w_in[l, here] = raw[here].reshape(group, 2 * half)

        load_down[l].wait()
        if l == 0:
            load_in[1].start()

    def compute(l, s, i):
        q, b = 2 * l + s, order[i]
        for j in range(2):
            spot = block(l, s, b, 2 + j)
            remote(spot, spot, c_send.at[q, i, j], c_recv.at[q, i, j], c_peer).wait_recv()
        count = 4 * size
        marks = rows1[s, b, :, :, width:].reshape(count, LANES).astype(f32)
        spots = lax.broadcasted_iota(jnp.int32, (count, LANES), 1)
        hit = (spots == lanes[l]) | (spots == lanes[l] + experts)
        weight = jnp.sum(jnp.where(hit, marks, 0.0), axis=1, keepdims=True)
        step = half

        @pl.loop(0, half // step)
        def _(j):
            x = rows[l][s, b, :, :, :width].reshape(count, width)
            here = pl.multiple_of(j * step, step)
            gate = jnp.dot(x, w_in[l, :, pl.ds(here, step)], preferred_element_type=f32)
            up = jnp.dot(x, w_in[l, :, pl.ds(half + here, step)], preferred_element_type=f32)
            hidden[:, pl.ds(here, step)] = (gate / (1.0 + jnp.exp(-gate)) * up).astype(bf16)

        y = jnp.dot(hidden[...], w_down[l], preferred_element_type=f32)
        y = jnp.where(weight == 0.0, 0.0, y * weight)
        part[q, i] = y.astype(bf16).reshape(4, size, width)
        go(remote(part.at[q, i, pl.ds(2, 2)], core_in.at[q, i], rc_send.at[q, i], rc_recv.at[q, i], c_peer))

    def pair_sum(q, i, j, p):
        return part[q, i, j, at[p]].astype(f32) + core_in[q, i, j, at[p]].astype(f32)

    def z_wait(q, slot, j, p):
        spot = z_in.at[q, slot, j, at[p]]
        remote(spot, spot, rz_send.at[q, 0, j, p], rz_recv.at[q, slot, j, p], {"ep": pair}).wait_recv()

    def line(q, i, j, p, value):
        slot_in = {1: 4, 2: 2, 3: 3}[i]
        slot_inner = {1: 0, 2: 1, 3: 4}[i]
        slot_outer = {1: 0, 2: 2, 3: 3}[i]
        slot = slot_inner if slot_inner == slot_outer else jnp.where(inner, slot_inner, slot_outer)
        to = pair if i == 1 else jnp.where(inner, other, pair)

        @pl.when(inner)
        def _():
            z_wait(q, slot_in, j, p)
            cross[q, i, j, at[p]] = (value() + z_in[q, slot_in, j, at[p]].astype(f32)).astype(bf16)

        @pl.when(outer)
        def _():
            cross[q, i, j, at[p]] = value().astype(bf16)

        go(
            remote(
                cross.at[q, i, j, at[p]], z_in.at[q, slot, j, at[p]], rz_send.at[q, i, j, p], rz_recv.at[q, slot, j, p],
                {"ep": to},
            )
        )

    def rx_go(q, i, p):
        go(
            remote(cross.at[q, i, 1, at[p]], x_in.at[q, i, at[p]], rx_send.at[q, i, p], rx_recv.at[q, i, p], x_peer)
        )

    def rx_wait(q, i, p):
        spot = x_in.at[q, i, at[p]]
        remote(spot, spot, rx_send.at[q, i, p], rx_recv.at[q, i, p], x_peer).wait_recv()

    def core_arrive(l, s, i):
        q = 2 * l + s
        remote(core_in.at[q, i], core_in.at[q, i], rc_send.at[q, i], rc_recv.at[q, i], c_peer).wait_recv()
        if REDUCE[l][s] == "z":
            for p in range(PIECES):
                cross[q, i, 1, at[p]] = pair_sum(q, i, 1, p).astype(bf16)
                rx_go(q, i, p)

    def total(j, l, s, i):
        q = 2 * l + s
        if REDUCE[l][s] == "z":
            for p in range(PIECES if j == 0 else 0):
                rx_wait(q, i, p)
                if i > 0:
                    line(q, i, 0, p, lambda: pair_sum(q, i, 0, p) + x_in[q, i, at[p]].astype(f32))
        elif i > 0:
            for p in range(PIECES):
                line(q, i, j, p, lambda: pair_sum(q, i, j, p))

    def gathered(q, j, p, value):
        z_wait(q, 0, j, p)
        pl.when(inner)(functools.partial(z_wait, q, 1, j, p))
        value = value + z_in[q, 0, j, at[p]].astype(f32)
        return value + jnp.where(inner, z_in[q, 1, j, at[p]].astype(f32), 0.0)

    def swap(l, s):
        q = 2 * l + s
        if REDUCE[l][s] == "x":
            for p in range(PIECES):
                cross[q, 0, 1, at[p]] = gathered(q, 1, p, pair_sum(q, 0, 1, p)).astype(bf16)
                rx_go(q, 0, p)

    def finish(l, s):
        q = 2 * l + s
        for p in range(PIECES):
            value = gathered(q, 0, p, pair_sum(q, 0, 0, p))
            if REDUCE[l][s] == "x":
                rx_wait(q, 0, p)
            value = value + x_in[q, 0, at[p]].astype(f32)
            here = pl.ds(s * size + p * cut, cut)
            if l == 0:
                now = (tokens[here].astype(f32) + value).astype(bf16)
                mixed[here] = now
                wide = now.astype(f32)
                inv_rms = lax.rsqrt(jnp.mean(wide * wide, axis=1, keepdims=True) + 1e-06)
                rows2[s, z, 0, at[p]] = (wide * inv_rms * gain_ref[...]).astype(bf16)
            else:
                out[here] = (mixed[here].astype(f32) + value).astype(bf16)
        if l == 0:
            start(1, s)

    steps = {
        "S": start, "W": weights, "a": functools.partial(arrive, 0),
        "b": functools.partial(arrive, 1), "x": x_arrive, "C": compute, "k": core_arrive, "t": functools.partial(total, 0), "u": functools.partial(total, 1), "f": swap,
        "F": finish,
    }
    for word in " ".join(PROGRAM).split():
        steps[word[0]](*[int(c) for c in word[1:]])
    for copy, when in sends:
        if when is None:
            copy.wait_send()
        else:
            pl.when(when)(copy.wait_send)


def fused_shards(
    tokens, experts_one, gates_one, w_in_one, w_down_one, norm_gain,
    experts_two, gates_two, placement_two, w_in_two, w_down_two,
):
    experts = placement_two.shape[0]
    tok, width = tokens.shape
    half = w_down_one.shape[1]
    n = lax.axis_size("ep")
    bf16 = jnp.bfloat16
    dma = pltpu.SemaphoreType.DMA
    size = tok // STREAMS
    q = 2 * STREAMS
    vmem = pl.BlockSpec(memory_space=pltpu.VMEM)
    hbm = pl.BlockSpec(memory_space=pl.ANY)
    top = experts_one.shape[1]
    return pl.pallas_call(
        functools.partial(fused_kernel, n, experts, width),
        out_shape=jax.ShapeDtypeStruct((tok, width), bf16),
        in_specs=[hbm] * 5 + [vmem, pl.BlockSpec(memory_space=pltpu.SMEM)] + [hbm] * 4,
        out_specs=vmem,
        scratch_shapes=[
            pltpu.VMEM((tok, width), bf16),
            pltpu.VMEM((2, top, tok), jnp.int32),
            pltpu.VMEM((2, top, tok), jnp.float32),
            pltpu.VMEM((tok, width), bf16),
            pltpu.VMEM((STREAMS, n, 4, size, width + LANES), bf16),
            pltpu.VMEM((STREAMS, n, 4, size, width), bf16),
            pltpu.VMEM((q, n, 4, size, width), bf16),
            pltpu.VMEM((q, n, 2, size, width), bf16),
            pltpu.VMEM((q, n, 2, size, width), bf16),
            pltpu.VMEM((q, n, size, width), bf16),
            pltpu.VMEM((q, 5, 2, size, width), bf16),
            pltpu.VMEM((width, 2, half), bf16),
            pltpu.VMEM((2, width, 2 * half), bf16),
            pltpu.VMEM((2, half, width), bf16),
            pltpu.VMEM((4 * size, half), bf16),
            dma((9,)),
            dma((q, 5, 2, PIECES)),
            dma((q, n, 2, PIECES)),
            dma((q, n, PIECES)),
            dma((q, n, PIECES)),
            dma((q, n, 2)),
            dma((q, n, 2)),
            dma((q, n)),
            dma((q, n)),
            dma((q, n, PIECES)),
            dma((q, n, PIECES)),
            dma((q, n, 2, PIECES)),
            dma((q, 5, 2, PIECES)),
        ],
        compiler_params=pltpu.CompilerParams(
            collective_id=0, has_side_effects=True, vmem_limit_bytes=63 * 1000 * 1000
        ),
        name="layers",
    )(
        tokens, experts_one.T, gates_one.T, experts_two.T, gates_two.T, norm_gain.reshape(1, width), placement_two,
        w_in_one.reshape(width, 2, half), w_down_one.reshape(half, width),
        w_in_two.reshape(width, 2, half), w_down_two.reshape(half, width),
    )


def capacity(tok_rows, top_count, expert_count):
    return max(2, min(tok_rows, 5 * tok_rows * top_count // (4 * expert_count)))


def pack_rows(rows_in, targets, expert_count, per_slot):
    tok_rows, top_count = targets.shape
    flat_ids = targets.reshape(-1)
    hit_table = (flat_ids[:, None] == jnp.arange(expert_count, dtype=jnp.int32)[None, :]).astype(
        jnp.int32
    )
    before = jnp.cumsum(hit_table, axis=0) - hit_table
    slot_rank = jnp.sum(before * hit_table, axis=1)
    slot_index = flat_ids * per_slot + slot_rank
    source = jnp.arange(tok_rows * top_count, dtype=jnp.int32) // top_count
    owner_row = jnp.zeros((expert_count * per_slot,), jnp.int32).at[slot_index].set(source)
    filled = jnp.zeros((expert_count * per_slot,), jnp.int32).at[slot_index].set(1)
    buffer = jnp.where(filled[:, None] > 0, rows_in[owner_row], jnp.zeros((), rows_in.dtype))
    return (buffer, slot_index)


def to_experts(buffer, expert_count, per_slot):
    row_width = buffer.shape[1]
    arrived = lax.all_to_all(
        buffer.reshape(expert_count, per_slot, row_width),
        ("ep", "dp"),
        split_axis=0,
        concat_axis=0,
        tiled=True,
    )
    return arrived.reshape(expert_count * per_slot, row_width)


def to_owners(produced, expert_count, per_slot):
    row_width = produced.shape[1]
    returned = lax.all_to_all(
        produced.reshape(expert_count, per_slot, row_width),
        ("ep", "dp"),
        split_axis=0,
        concat_axis=0,
        tiled=True,
    )
    return returned.reshape(expert_count * per_slot, row_width)


def run_expert(received, w_in, w_down):
    row_width = received.shape[1]
    down_local = w_down[0]
    half_width = down_local.shape[0]
    w_local = w_in.reshape(row_width, 2 * half_width)
    gate_up = jnp.dot(
        lax.all_gather(received, "tp", axis=0, tiled=True),
        w_local,
        preferred_element_type=jnp.float32,
    )
    hidden = (jax.nn.silu(gate_up[:, :half_width]) * gate_up[:, half_width:]).astype(jnp.bfloat16)
    return lax.psum_scatter(
        jnp.dot(hidden, down_local, preferred_element_type=jnp.float32).astype(jnp.bfloat16),
        "tp",
        scatter_dimension=0,
        tiled=True,
    )


def moe_block(rows_in, targets, gate_values, w_in, w_down, expert_count, per_slot):
    tok_rows, top_count = targets.shape
    row_width = rows_in.shape[1]
    buffer, slot_index = pack_rows(rows_in, targets, expert_count, per_slot)
    arrived = to_experts(buffer, expert_count, per_slot)
    produced = run_expert(arrived, w_in, w_down)
    returned = to_owners(produced, expert_count, per_slot)
    picked = returned[slot_index].reshape(tok_rows, top_count, row_width)
    return jnp.sum(gate_values[:, :, None] * picked.astype(jnp.float32), axis=1)


def shards(
    tokens,
    experts_one,
    gates_one,
    w_in_one,
    w_down_one,
    norm_gain,
    experts_two,
    gates_two,
    placement_two,
    w_in_two,
    w_down_two,
):
    tok_rows, top_count = experts_one.shape
    expert_count = placement_two.shape[0]
    per_slot = capacity(tok_rows, top_count, expert_count)
    moe_one = moe_block(
        tokens, experts_one, gates_one, w_in_one, w_down_one, expert_count, per_slot
    )
    mixed = (tokens.astype(jnp.float32) + moe_one).astype(jnp.bfloat16)
    mixed = lax.optimization_barrier(mixed)
    mixed_wide = mixed.astype(jnp.float32)
    inv_rms = lax.rsqrt(jnp.mean(mixed_wide * mixed_wide, axis=1, keepdims=True) + 1e-06)
    normed = (mixed_wide * inv_rms * norm_gain[None, :]).astype(jnp.bfloat16)
    expert_range = jnp.arange(expert_count, dtype=jnp.int32)
    matches = experts_two[:, :, None] == expert_range[None, None, :]
    layer_slots = jnp.sum(jnp.where(matches, placement_two[None, None, :], 0), axis=2)
    moe_two = moe_block(
        normed, layer_slots, gates_two, w_in_two, w_down_two, expert_count, per_slot
    )
    return (mixed_wide + moe_two).astype(jnp.bfloat16)


def solution(mesh):
    in_specs = (
        P(("groups", "ep", "dp", "tp"), None),
        P(("groups", "ep", "dp", "tp"), None),
        P(("groups", "ep", "dp", "tp"), None),
        P(("ep", "dp"), None, None, "tp"),
        P(("ep", "dp"), "tp", None),
        P(),
        P(("groups", "ep", "dp", "tp"), None),
        P(("groups", "ep", "dp", "tp"), None),
        P(),
        P(("ep", "dp"), None, None, "tp"),
        P(("ep", "dp"), "tp", None),
    )
    out_specs = P(("groups", "ep", "dp", "tp"), None)
    ready = mesh.shape["tp"] == 1 and mesh.shape["dp"] == 4 and mesh.shape["ep"] == 4

    def body(*arrays):
        return (fused_shards if ready and arrays[0].shape[0] % 32 == 0 else shards)(*arrays)

    return jax.shard_map(body, mesh=mesh, in_specs=in_specs, out_specs=out_specs, check_vma=False)
```

time: 142 us -> 112 us (0.79)
  Pallas kernels: 134 us -> 110 us
  other arithmetic: 5.44 us -> 0 us
    pallas_call x2 -> x1, Pallas kernels: 134 us -> 110 us  [fused_shards(): pl.pallas_call(functools.partial(fused_kernel, n, experts, width), out_sh...]
    reduce_sum x4 -> x0, other arithmetic: 3.48 us -> none  [the longest x2 1.43 us: with_gates(): table = jnp.sum(jnp.where(matches, gate_values[:, :, None], 0.0), axis=1)]
    concatenate x2 -> x0, local copies, waits for them, and re-layouts: 2.55 us -> none  [with_gates(): return jnp.concatenate([rows_in, high, low, rest], axis=1)]
    convert_element_type x6 -> x0, other arithmetic: 1.95 us -> none  [the longest x1 1.79 us: fused_shards(): return (mixed_wide + moe_two).astype(jnp.bfloat16)]
    unnamed x4 -> x1, local copies, waits for them, and re-layouts: 0.01 us -> 1.67 us
where the time goes in v1:
time: 112 us
  Pallas kernels  110 us (98%)
  local copies, waits for them, and re-layouts  1.67 us (1%)
    pallas_call x1, Pallas kernels, fused_shards(): pl.pallas_call(functools.partial(fused_kernel, n, experts, width), out_sh...  110 us

profile of v1, /device:TPU:0, one launch (start us, length us, event | category | flops | bytes accessed | tf_op | source)
XLA Modules:
  0.0 111.6 jit_solution(7130578297149411030)
XLA Ops:
  0.0 109.9 %layers.1 = bf16[64,2048]{1,0:T(8,128)(2,1)} custom-call(bf16[64,2048]{1,0:T(8,128)(2,1)} %tokens_hbm.1, s32[8,64]{1,0:T(8,128)} %bitcast.14, f32[8,64]{1,0:T(8,128)} %bitcast.15, s32[8,64]{1,0:T(8,128)} %bitcast.16, f32[8,64]{1,0:T(8,128)} %bitcast.17, f32[1,2048]{1,0:T(1,128)} %bitcast.13, s32[16]{0:T(128)} %place.1, bf16[2048,2,768]{2,1,0:T(2,128)(2,1)} %bitcast.9, ...), custom_call_target="tpu_custom_call" | custom-call | tf_op jit(solution)/shard_map/layers/pallas_call | solution.py:345
  109.9 1.7 %copy.13 = bf16[64,2048]{1,0:T(8,128)(2,1)} copy(bf16[64,2048]{1,0:T(8,128)(2,1)} %layers.1) | data formatting | bytes 524288

commit v2 on v1

--- a/solution.py
+++ b/solution.py
@@ -13,37 +13,73 @@
 
 STREAMS = 2
 PIECES = 2
-GATHER = ('zx', 'zx')
-REDUCE = ('zz', 'zz')
-PROGRAM = (
-    "S00 W0 S01 W1",
-    "x000 a002 a001 x010",
-    "a011 C000 a003 x002",
-    "C010 k000 C002 x001",
-    "b012 k010 b011 x003",
-    "k002 a012 C001 C003",
-    "a013 C012 k003 b013",
-    "t002 k012 k001 C013",
-    "t003 C011 t012 t000",
-    "k013 t001 k011 t013",
-    "F00 t011 t010 a101",
-    "x100 a102 F01 x101",
-    "C101 x102 a103 C100",
-    "x110 C102 x103 k101",
-    "a111 a112 k100 C103",
-    "b112 k103 a113 b111",
-    "C112 k102 b113 t103",
-    "k112 C113 t102 t101",
-    "k113 C111 C110 k111",
-    "t100 t113 k110 t112",
-    "t111 F10 t110 F11",
+GATHER = ("zx", "zx")
+REDUCE = ("zz", "xz")
+OUTER = (
+    "S00 S01 x000 W0",
+    "a002 x010 a001 C000",
+    "C010 x002 a003 C002",
+    "k000 x003 a011 k002",
+    "x001 C003 b011 C001",
+    "k003 t002 C011 b013",
+    "k001 k010 t000 a013",
+    "t003 a012 C013 t001",
+    "b012 k013 k011 C012",
+    "t013 t010 k012 F00",
+    "t012 a101 W1 t011",
+    "a102 x100 F01 x101",
+    "a103 x102 C101 x110",
+    "C102 x103 k102 t102",
+    "C103 u102 C100 C110",
+    "k103 b111 k101 a111",
+    "u103 a113 k110 t103",
+    "b113 t101 a112 C113",
+    "b112 C111 k100 k113",
+    "t110 u101 C112 t113",
+    "k112 k111 t112 f10",
+    "t111 F10 F11",
 )
+INNER = (
+    "S00 a002 a001 x000",
+    "S01 W0 C000 x002",
+    "a003 a012 b011 x001",
+    "a011 C002 x010 k000",
+    "k002 x003 b013 C011",
+    "C003 a013 k011 C001",
+    "k003 C010 b012 C013",
+    "t002 k001 k010 t003",
+    "k013 C012 t001 k012",
+    "t010 t000 F00 t013",
+    "a102 a101 t011 x100",
+    "t012 a103 F01 W1",
+    "a111 a112 x110 x103",
+    "x101 x102 a113 b111",
+    "C101 C102 b113 b112",
+    "C103 k101 C113 k102",
+    "t102 k103 C111 u103",
+    "C110 k113 t103 C100",
+    "k110 k111 C112 u102",
+    "t101 u101 t113 t110",
+    "k100 k112 f10 t111",
+    "t112 F10 F11",
+)
+
+
+def segments(lines):
+    parts, calls = [[]], []
+    for word in " ".join(lines).split():
+        if word[0] == "C":
+            calls.append([int(c) for c in word[1:]])
+            parts.append([])
+        else:
+            parts[-1].append(word)
+    return parts, calls
 
 
 def fused_kernel(
     n, experts, width, tokens_hbm, experts_hbm, gates_hbm, experts2_hbm, gates2_hbm, gain_ref, place, w_in1, w_down1,
     w_in2, w_down2, out, tokens, ids, gates, mixed, rows1, rows2, part, core_in, cross, x_in, z_in, raw, w_in, w_down,
-    hidden, w_sem, z_send, z_recv, x_send, x_recv, c_send, c_recv, rc_send, rc_recv, rx_send, rx_recv, rz_send, rz_recv,
+    hidden, gate_up, w_sem, z_send, z_recv, x_send, x_recv, c_send, c_recv, rc_send, rc_recv, rx_send, rx_recv, rz_send, rz_recv,
 ):
     z = lax.axis_index("ep")
     d = lax.axis_index("dp")
@@ -91,14 +127,12 @@
     def _():
         pl.semaphore_signal(barrier, inc=1, device_id={"ep": other}, device_id_type=MESH)
 
-    sends = []
-
-    def go(copy, when=None):
-        if when is None:
-            copy.start()
-        else:
-            pl.when(when)(copy.start)
-        sends.append((copy, when))
+    common = []
+    sends = {False: [], True: []}
+
+    def go(make, ins=None):
+        make().start()
+        (common if ins is None else sends[ins]).append(make)
 
     for copy in small:
         copy.wait()
@@ -130,62 +164,60 @@
     def block(l, s, b, j):
         return rows[l].at[s, b, j]
 
-    def z_own(l, s, j):
+    def z_move(l, s, b, j, p, k, to):
         q = 2 * l + s
-        for p in range(PIECES):
-            spot = block(l, s, z, j).at[at[p]]
-            up = remote(spot, spot, z_send.at[q, 0, j, p], z_recv.at[q, z, j, p], {"ep": pair})
-            go(up)
-            down = remote(spot, spot, z_send.at[q, 1, j, p], z_recv.at[q, z, j, p], {"ep": other})
-            go(down, inner)
-
-    def x_move(l, s, i):
+        spot = block(l, s, b, j).at[at[p]]
+        return remote(spot, spot, z_send.at[q, k, j, p], z_recv.at[q, b, j, p], {"ep": to})
+
+    def z_own(ins, l, s, j):
+        for p in range(PIECES):
+            go(functools.partial(z_move, l, s, z, j, p, 0, pair), ins)
+            if ins:
+                go(functools.partial(z_move, l, s, z, j, p, 1, other), ins)
+
+    def x_move(ins, l, s, i, p):
         q, b = 2 * l + s, order[i]
-        for p in range(PIECES):
-            go(
-                remote(
-                    block(l, s, b, 0).at[at[p]], block(l, s, b, 1).at[at[p]], x_send.at[q, i, p], x_recv.at[q, i, p], x_peer
-                )
-            )
-
-    def c_move(l, s, i, j):
+
+        def make():
+            spot, there = block(l, s, b, 0).at[at[p]], block(l, s, b, 1).at[at[p]]
+            return remote(spot, there, x_send.at[q, i, p], x_recv.at[q, i, p], x_peer)
+
+        go(make, ins)
+
+    def c_move(ins, l, s, i, j):
         q, b = 2 * l + s, order[i]
-        go(remote(block(l, s, b, j), block(l, s, b, 2 + j), c_send.at[q, i, j], c_recv.at[q, i, j], c_peer))
-
-    def start(l, s):
-        z_own(l, s, 0)
-        x_move(l, s, 0)
-        c_move(l, s, 0, 0)
-
-    def arrive(j, l, s, i):
-        q, b = 2 * l + s, order[i]
-        to = {"ep": other if i == 1 else pair}
-        first = GATHER[l][s] == "z"
-        if first and j == 1:
-            return
-        for p in range(PIECES):
-            spot = block(l, s, b, j).at[at[p]]
-            move = remote(spot, spot, z_send.at[q, 1 + i, j, p], z_recv.at[q, b, j, p], to)
-            move.wait_recv()
-            go(move, inner)
-            if first:
-                go(
-                    remote(spot, block(l, s, b, 1).at[at[p]], x_send.at[q, i, p], x_recv.at[q, i, p], x_peer)
-                )
-        c_move(l, s, i, j)
-
-    def x_arrive(l, s, i):
-        if GATHER[l][s] == "x" and i > 0:
-            return
+
+        def make():
+            return remote(block(l, s, b, j), block(l, s, b, 2 + j), c_send.at[q, i, j], c_recv.at[q, i, j], c_peer)
+
+        go(make, ins)
+
+    def start(ins, l, s):
+        z_own(ins, l, s, 0)
+        for p in range(PIECES):
+            x_move(ins, l, s, 0, p)
+        c_move(ins, l, s, 0, 0)
+
+    def arrive(j, ins, l, s, i):
+        for p in range(PIECES):
+            move = functools.partial(z_move, l, s, order[i], j, p, 1 + i, other if i == 1 else pair)
+            move().wait_recv()
+            if ins:
+                go(move, ins)
+            if GATHER[l][s] == "z":
+                x_move(ins, l, s, i, p)
+        c_move(ins, l, s, i, j)
+
+    def x_arrive(ins, l, s, i):
         q, b = 2 * l + s, order[i]
         for p in range(PIECES):
             spot = block(l, s, b, 1).at[at[p]]
             remote(spot, spot, x_send.at[q, i, p], x_recv.at[q, i, p], x_peer).wait_recv()
         if GATHER[l][s] == "x":
-            z_own(l, s, 1)
-        c_move(l, s, i, 1)
-
-    def weights(l):
+            z_own(ins, l, s, 1)
+        c_move(ins, l, s, i, 1)
+
+    def weights(ins, l):
         load_in[l].wait()
         group = 128
 
@@ -198,8 +230,14 @@
         if l == 0:
             load_in[1].start()
 
-    def compute(l, s, i):
-        q, b = 2 * l + s, order[i]
+    def pick(a, b):
+        return a if a is b or isinstance(a, int) and isinstance(b, int) and a == b else jnp.where(inner, b, a)
+
+    def compute(l, outer_at, inner_at):
+        s = pick(outer_at[0], inner_at[0])
+        i = pick(outer_at[1], inner_at[1])
+        b = pick(order[outer_at[1]], order[inner_at[1]])
+        q = 2 * l + s
         for j in range(2):
             spot = block(l, s, b, 2 + j)
             remote(spot, spot, c_send.at[q, i, j], c_recv.at[q, i, j], c_peer).wait_recv()
@@ -208,20 +246,23 @@
         spots = lax.broadcasted_iota(jnp.int32, (count, LANES), 1)
         hit = (spots == lanes[l]) | (spots == lanes[l] + experts)
         weight = jnp.sum(jnp.where(hit, marks, 0.0), axis=1, keepdims=True)
-        step = half
-
-        @pl.loop(0, half // step)
+
+        @pl.loop(0, 2)
         def _(j):
             x = rows[l][s, b, :, :, :width].reshape(count, width)
-            here = pl.multiple_of(j * step, step)
-            gate = jnp.dot(x, w_in[l, :, pl.ds(here, step)], preferred_element_type=f32)
-            up = jnp.dot(x, w_in[l, :, pl.ds(half + here, step)], preferred_element_type=f32)
-            hidden[:, pl.ds(here, step)] = (gate / (1.0 + jnp.exp(-gate)) * up).astype(bf16)
-
+            here = pl.multiple_of(j * half, LANES)
+            gate_up[j] = jnp.dot(x, w_in[l, :, pl.ds(here, half)], preferred_element_type=f32)
+
+        gate = gate_up[0]
+        hidden[...] = (gate / (1.0 + jnp.exp(-gate)) * gate_up[1]).astype(bf16)
         y = jnp.dot(hidden[...], w_down[l], preferred_element_type=f32)
         y = jnp.where(weight == 0.0, 0.0, y * weight)
         part[q, i] = y.astype(bf16).reshape(4, size, width)
-        go(remote(part.at[q, i, pl.ds(2, 2)], core_in.at[q, i], rc_send.at[q, i], rc_recv.at[q, i], c_peer))
+
+        def make():
+            return remote(part.at[q, i, pl.ds(2, 2)], core_in.at[q, i], rc_send.at[q, i], rc_recv.at[q, i], c_peer)
+
+        go(make)
 
     def pair_sum(q, i, j, p):
         return part[q, i, j, at[p]].astype(f32) + core_in[q, i, j, at[p]].astype(f32)
@@ -230,74 +271,68 @@
         spot = z_in.at[q, slot, j, at[p]]
         remote(spot, spot, rz_send.at[q, 0, j, p], rz_recv.at[q, slot, j, p], {"ep": pair}).wait_recv()
 
-    def line(q, i, j, p, value):
-        slot_in = {1: 4, 2: 2, 3: 3}[i]
-        slot_inner = {1: 0, 2: 1, 3: 4}[i]
-        slot_outer = {1: 0, 2: 2, 3: 3}[i]
-        slot = slot_inner if slot_inner == slot_outer else jnp.where(inner, slot_inner, slot_outer)
-        to = pair if i == 1 else jnp.where(inner, other, pair)
-
-        @pl.when(inner)
-        def _():
+    def line(ins, q, i, j, p, value):
+        if ins:
+            slot_in = {1: 4, 2: 2, 3: 3}[i]
             z_wait(q, slot_in, j, p)
-            cross[q, i, j, at[p]] = (value() + z_in[q, slot_in, j, at[p]].astype(f32)).astype(bf16)
-
-        @pl.when(outer)
-        def _():
-            cross[q, i, j, at[p]] = value().astype(bf16)
-
-        go(
-            remote(
-                cross.at[q, i, j, at[p]], z_in.at[q, slot, j, at[p]], rz_send.at[q, i, j, p], rz_recv.at[q, slot, j, p],
-                {"ep": to},
-            )
-        )
-
-    def rx_go(q, i, p):
-        go(
-            remote(cross.at[q, i, 1, at[p]], x_in.at[q, i, at[p]], rx_send.at[q, i, p], rx_recv.at[q, i, p], x_peer)
-        )
+            value = value + z_in[q, slot_in, j, at[p]].astype(f32)
+        slot = {1: 0, 2: 1, 3: 4}[i] if ins else {1: 0, 2: 2, 3: 3}[i]
+        to = other if ins and i > 1 else pair
+        cross[q, i, j, at[p]] = value.astype(bf16)
+
+        def make():
+            spot, there = cross.at[q, i, j, at[p]], z_in.at[q, slot, j, at[p]]
+            return remote(spot, there, rz_send.at[q, i, j, p], rz_recv.at[q, slot, j, p], {"ep": to})
+
+        go(make, ins)
+
+    def rx_go(ins, q, i, p):
+        def make():
+            spot, there = cross.at[q, i, 1, at[p]], x_in.at[q, i, at[p]]
+            return remote(spot, there, rx_send.at[q, i, p], rx_recv.at[q, i, p], x_peer)
+
+        go(make, ins)
 
     def rx_wait(q, i, p):
         spot = x_in.at[q, i, at[p]]
         remote(spot, spot, rx_send.at[q, i, p], rx_recv.at[q, i, p], x_peer).wait_recv()
 
-    def core_arrive(l, s, i):
+    def core_arrive(ins, l, s, i):
         q = 2 * l + s
         remote(core_in.at[q, i], core_in.at[q, i], rc_send.at[q, i], rc_recv.at[q, i], c_peer).wait_recv()
         if REDUCE[l][s] == "z":
             for p in range(PIECES):
                 cross[q, i, 1, at[p]] = pair_sum(q, i, 1, p).astype(bf16)
-                rx_go(q, i, p)
-
-    def total(j, l, s, i):
+                rx_go(ins, q, i, p)
+
+    def total(j, ins, l, s, i):
         q = 2 * l + s
-        if REDUCE[l][s] == "z":
-            for p in range(PIECES if j == 0 else 0):
+        for p in range(PIECES):
+            if REDUCE[l][s] == "z":
                 rx_wait(q, i, p)
-                if i > 0:
-                    line(q, i, 0, p, lambda: pair_sum(q, i, 0, p) + x_in[q, i, at[p]].astype(f32))
-        elif i > 0:
-            for p in range(PIECES):
-                line(q, i, j, p, lambda: pair_sum(q, i, j, p))
-
-    def gathered(q, j, p, value):
-        z_wait(q, 0, j, p)
-        pl.when(inner)(functools.partial(z_wait, q, 1, j, p))
-        value = value + z_in[q, 0, j, at[p]].astype(f32)
-        return value + jnp.where(inner, z_in[q, 1, j, at[p]].astype(f32), 0.0)
-
-    def swap(l, s):
+            if i > 0:
+                value = pair_sum(q, i, j, p)
+                if REDUCE[l][s] == "z":
+                    value = value + x_in[q, i, at[p]].astype(f32)
+                line(ins, q, i, j, p, value)
+
+    def gathered(ins, q, j, p):
+        value = pair_sum(q, 0, j, p)
+        for slot in range(2 if ins else 1):
+            z_wait(q, slot, j, p)
+            value = value + z_in[q, slot, j, at[p]].astype(f32)
+        return value
+
+    def swap(ins, l, s):
         q = 2 * l + s
-        if REDUCE[l][s] == "x":
-            for p in range(PIECES):
-                cross[q, 0, 1, at[p]] = gathered(q, 1, p, pair_sum(q, 0, 1, p)).astype(bf16)
-                rx_go(q, 0, p)
-
-    def finish(l, s):
+        for p in range(PIECES):
+            cross[q, 0, 1, at[p]] = gathered(ins, q, 1, p).astype(bf16)
+            rx_go(ins, q, 0, p)
+
+    def finish(ins, l, s):
         q = 2 * l + s
         for p in range(PIECES):
-            value = gathered(q, 0, p, pair_sum(q, 0, 0, p))
+            value = gathered(ins, q, 0, p)
             if REDUCE[l][s] == "x":
                 rx_wait(q, 0, p)
             value = value + x_in[q, 0, at[p]].astype(f32)
@@ -311,20 +346,34 @@
             else:
                 out[here] = (mixed[here].astype(f32) + value).astype(bf16)
         if l == 0:
-            start(1, s)
+            start(ins, 1, s)
 
     steps = {
-        "S": start, "W": weights, "a": functools.partial(arrive, 0),
-        "b": functools.partial(arrive, 1), "x": x_arrive, "C": compute, "k": core_arrive, "t": functools.partial(total, 0), "u": functools.partial(total, 1), "f": swap,
-        "F": finish,
+        "S": start, "W": weights, "x": x_arrive, "k": core_arrive, "f": swap, "F": finish,
+        "a": functools.partial(arrive, 0), "b": functools.partial(arrive, 1),
+        "t": functools.partial(total, 0), "u": functools.partial(total, 1),
     }
-    for word in " ".join(PROGRAM).split():
-        steps[word[0]](*[int(c) for c in word[1:]])
-    for copy, when in sends:
-        if when is None:
-            copy.wait_send()
-        else:
-            pl.when(when)(copy.wait_send)
+
+    def run(ins, words):
+        for word in words:
+            steps[word[0]](ins, *[int(c) for c in word[1:]])
+
+    plans = {False: segments(OUTER), True: segments(INNER)}
+    for k in range(len(plans[True][0])):
+        for ins, when in ((False, outer), (True, inner)):
+            if plans[ins][0][k]:
+                pl.when(when)(functools.partial(run, ins, plans[ins][0][k]))
+        if k < len(plans[True][1]):
+            (l, *outer_at), (_, *inner_at) = plans[False][1][k], plans[True][1][k]
+            compute(l, outer_at, inner_at)
+    for make in common:
+        make().wait_send()
+    for ins, when in ((False, outer), (True, inner)):
+
+        @pl.when(when)
+        def _(ins=ins):
+            for make in sends[ins]:
+                make().wait_send()
 
 
 def fused_shards(
@@ -363,6 +412,7 @@
             pltpu.VMEM((2, width, 2 * half), bf16),
             pltpu.VMEM((2, half, width), bf16),
             pltpu.VMEM((4 * size, half), bf16),
+            pltpu.VMEM((2, 4 * size, half), jnp.float32),
             dma((9,)),
             dma((q, 5, 2, PIECES)),
             dma((q, n, 2, PIECES)),

time: 112 us -> 101 us (0.902)
  Pallas kernels: 110 us -> 98.5 us
    pallas_call x1, Pallas kernels: 110 us -> 98.5 us  [fused_shards(): pl.pallas_call(functools.partial(fused_kernel, n, experts, width), out_sh...]
where the time goes in v2:
time: 101 us; the launch traced here: 100 us
  Pallas kernels  98.5 us (98%)
  local copies, waits for them, and re-layouts  1.67 us (2%)
    pallas_call x1, Pallas kernels, fused_shards(): pl.pallas_call(functools.partial(fused_kernel, n, experts, width), out_sh...  98.5 us

profile of v2, /device:TPU:0, one launch (start us, length us, event | category | flops | bytes accessed | tf_op | source)
XLA Modules:
  0.0 100.2 jit_solution(12137523086108214087)
XLA Ops:
  0.0 98.5 %layers.1 = bf16[64,2048]{1,0:T(8,128)(2,1)} custom-call(bf16[64,2048]{1,0:T(8,128)(2,1)} %tokens_hbm.1, s32[8,64]{1,0:T(8,128)} %bitcast.14, f32[8,64]{1,0:T(8,128)} %bitcast.15, s32[8,64]{1,0:T(8,128)} %bitcast.16, f32[8,64]{1,0:T(8,128)} %bitcast.17, f32[1,2048]{1,0:T(1,128)} %bitcast.13, s32[16]{0:T(128)} %place.1, bf16[2048,2,768]{2,1,0:T(2,128)(2,1)} %bitcast.9, ...), custom_call_target="tpu_custom_call" | custom-call | tf_op jit(solution)/shard_map/layers/pallas_call | solution.py:394
  98.5 1.7 %copy.13 = bf16[64,2048]{1,0:T(8,128)(2,1)} copy(bf16[64,2048]{1,0:T(8,128)(2,1)} %layers.1) | data formatting | bytes 524288

commit v3 on v2

--- a/solution.py
+++ b/solution.py
@@ -16,51 +16,51 @@
 GATHER = ("zx", "zx")
 REDUCE = ("zz", "xz")
 OUTER = (
-    "S00 S01 x000 W0",
-    "a002 x010 a001 C000",
-    "C010 x002 a003 C002",
-    "k000 x003 a011 k002",
-    "x001 C003 b011 C001",
-    "k003 t002 C011 b013",
-    "k001 k010 t000 a013",
-    "t003 a012 C013 t001",
-    "b012 k013 k011 C012",
-    "t013 t010 k012 F00",
-    "t012 a101 W1 t011",
-    "a102 x100 F01 x101",
-    "a103 x102 C101 x110",
-    "C102 x103 k102 t102",
-    "C103 u102 C100 C110",
-    "k103 b111 k101 a111",
-    "u103 a113 k110 t103",
-    "b113 t101 a112 C113",
-    "b112 C111 k100 k113",
-    "t110 u101 C112 t113",
-    "k112 k111 t112 f10",
-    "t111 F10 F11",
+    "S00 S01 a001 W0",
+    "x010 a002 x001 x000",
+    "C010 a003 x002 C001",
+    "C002 k001 x003 C000",
+    "k002 C003 a013 a011",
+    "b013 b011 k003 k000",
+    "t002 C013 t003 t001",
+    "k013 C011 a012 b012",
+    "k011 t013 t000 k010",
+    "C012 k012 F00 t012",
+    "t011 t010 a101 W1",
+    "F01 x101 x110 a103",
+    "C101 x100 C110 k101",
+    "a102 u101 t101 x103",
+    "C100 C103 k110 x102",
+    "k103 u103 a113 a111",
+    "C102 t110 b113 t103",
+    "k102 u102 a112 t102",
+    "C113 k113 b112 k100",
+    "b111 C112 t113 k112",
+    "C111 k111 t112 f10",
+    "t111 F11 F10",
 )
 INNER = (
-    "S00 a002 a001 x000",
-    "S01 W0 C000 x002",
-    "a003 a012 b011 x001",
-    "a011 C002 x010 k000",
-    "k002 x003 b013 C011",
-    "C003 a013 k011 C001",
-    "k003 C010 b012 C013",
-    "t002 k001 k010 t003",
-    "k013 C012 t001 k012",
-    "t010 t000 F00 t013",
-    "a102 a101 t011 x100",
-    "t012 a103 F01 W1",
-    "a111 a112 x110 x103",
-    "x101 x102 a113 b111",
-    "C101 C102 b113 b112",
-    "C103 k101 C113 k102",
-    "t102 k103 C111 u103",
-    "C110 k113 t103 C100",
-    "k110 k111 C112 u102",
-    "t101 u101 t113 t110",
-    "k100 k112 f10 t111",
+    "S00 W0 S01 a002",
+    "a001 a011 x000 a003",
+    "C000 a013 b011 x002",
+    "x010 x001 k000 C002",
+    "b013 x003 C010 k002",
+    "C001 k010 b012 C003",
+    "a012 C013 k003 C011",
+    "k001 t000 C012 k013",
+    "t003 k011 k012 t002",
+    "t001 t013 F00 W1",
+    "t011 t010 a101 a102",
+    "t012 a103 x101 F01",
+    "C101 a111 x100 a112",
+    "b111 x102 x103 a113",
+    "b113 x110 C103 C110",
+    "b112 C102 k103 u103",
+    "k110 C113 C111 t103",
+    "k102 C112 t110 k113",
+    "u102 k101 C100 u101",
+    "k111 t101 t113 t102",
+    "k112 k100 t111 f10",
     "t112 F10 F11",
 )
 
@@ -79,7 +79,7 @@
 def fused_kernel(
     n, experts, width, tokens_hbm, experts_hbm, gates_hbm, experts2_hbm, gates2_hbm, gain_ref, place, w_in1, w_down1,
     w_in2, w_down2, out, tokens, ids, gates, mixed, rows1, rows2, part, core_in, cross, x_in, z_in, raw, w_in, w_down,
-    hidden, gate_up, w_sem, z_send, z_recv, x_send, x_recv, c_send, c_recv, rc_send, rc_recv, rx_send, rx_recv, rz_send, rz_recv,
+    hidden, w_sem, z_send, z_recv, x_send, x_recv, c_send, c_recv, rc_send, rc_recv, rx_send, rx_recv, rz_send, rz_recv,
 ):
     z = lax.axis_index("ep")
     d = lax.axis_index("dp")
@@ -247,14 +247,10 @@
         hit = (spots == lanes[l]) | (spots == lanes[l] + experts)
         weight = jnp.sum(jnp.where(hit, marks, 0.0), axis=1, keepdims=True)
 
-        @pl.loop(0, 2)
-        def _(j):
-            x = rows[l][s, b, :, :, :width].reshape(count, width)
-            here = pl.multiple_of(j * half, LANES)
-            gate_up[j] = jnp.dot(x, w_in[l, :, pl.ds(here, half)], preferred_element_type=f32)
-
-        gate = gate_up[0]
-        hidden[...] = (gate / (1.0 + jnp.exp(-gate)) * gate_up[1]).astype(bf16)
+        x = rows[l][s, b, :, :, :width].reshape(count, width)
+        gate = jnp.dot(x, w_in[l, :, :half], preferred_element_type=f32)
+        up = jnp.dot(x, w_in[l, :, half:], preferred_element_type=f32)
+        hidden[...] = (gate / (1.0 + jnp.exp(-gate)) * up).astype(bf16)
         y = jnp.dot(hidden[...], w_down[l], preferred_element_type=f32)
         y = jnp.where(weight == 0.0, 0.0, y * weight)
         part[q, i] = y.astype(bf16).reshape(4, size, width)
@@ -412,7 +408,6 @@
             pltpu.VMEM((2, width, 2 * half), bf16),
             pltpu.VMEM((2, half, width), bf16),
             pltpu.VMEM((4 * size, half), bf16),
-            pltpu.VMEM((2, 4 * size, half), jnp.float32),
             dma((9,)),
             dma((q, 5, 2, PIECES)),
             dma((q, n, 2, PIECES)),

time: 101 us -> 98.4 us (0.974)
  Pallas kernels: 98.5 us -> 96.6 us
    pallas_call x1, Pallas kernels: 98.5 us -> 96.6 us  [fused_shards(): pl.pallas_call(functools.partial(fused_kernel, n, experts, width), out_sh...]
where the time goes in v3:
time: 98.4 us; the launch traced here: 98.2 us
  Pallas kernels  96.6 us (98%)
  local copies, waits for them, and re-layouts  1.67 us (2%)
    pallas_call x1, Pallas kernels, fused_shards(): pl.pallas_call(functools.partial(fused_kernel, n, experts, width), out_sh...  96.6 us

profile of v3, /device:TPU:0, one launch (start us, length us, event | category | flops | bytes accessed | tf_op | source)
XLA Modules:
  0.0 98.2 jit_solution(8600830177594888291)
XLA Ops:
  0.0 96.6 %layers.1 = bf16[64,2048]{1,0:T(8,128)(2,1)} custom-call(bf16[64,2048]{1,0:T(8,128)(2,1)} %tokens_hbm.1, s32[8,64]{1,0:T(8,128)} %bitcast.14, f32[8,64]{1,0:T(8,128)} %bitcast.15, s32[8,64]{1,0:T(8,128)} %bitcast.16, f32[8,64]{1,0:T(8,128)} %bitcast.17, f32[1,2048]{1,0:T(1,128)} %bitcast.13, s32[16]{0:T(128)} %place.1, bf16[2048,2,768]{2,1,0:T(2,128)(2,1)} %bitcast.9, ...), custom_call_target="tpu_custom_call" | custom-call | tf_op jit(solution)/shard_map/layers/pallas_call | solution.py:390
  96.6 1.7 %copy.13 = bf16[64,2048]{1,0:T(8,128)(2,1)} copy(bf16[64,2048]{1,0:T(8,128)(2,1)} %layers.1) | data formatting | bytes 524288
